TPU v7x, 32 devices: a whole 2x2x4 slice. The times are simulated.
32 devices in a mesh: row: 8 (over y, x, core), col: 4 (over z).
Axes of the slice: x: 2, y: 2, z: 4, core: 2. Of those that a mesh axis runs over, the one named last changes fastest.
Arguments:
- expression: bfloat16 [4096, 1024], P(('row', 'col')), may hold values from -200 to 200, as said below
- powers: int32 [10], replicated, may hold values from 1 to 20
Outputs:
- log_degree: float32 [10, 4096], P(None, ('row', 'col'))
- degree_freq: float32 [10, 10], replicated
- fit_slope: float32 [10], replicated
- mean_log: float32 [10], replicated
Inputs may be any that keep to these rules, and one draw needn't show every extreme that they name: Finite expression values.
All inputs are finite; a program needn't handle non-finite values.
Results may differ from a plain program's by a relative error of at most 0.0003.
Values may be sent and summed in bfloat16 or wider, within the bound.
A program may use at most 64 MiB of HBM per device.

v0:
```python
import functools
import math

import jax
import jax.numpy as jnp
from jax import lax
from jax.experimental import pallas as pl
from jax.experimental.pallas import tpu as pltpu
from jax.sharding import PartitionSpec as P

BINS = 10
HALVES = 2
LOG2E = math.log2(math.e)
LOG10E = math.log10(math.e)
MESH = pl.DeviceIdType.MESH


def xor(value, mask, size):
    result, bit = 0, 1
    while bit < size:
        one, two = (value // bit) % 2, (mask // bit) % 2
        result = result + bit * (one + two - 2 * one * two)
        bit *= 2
    return result


def gene_stats(block):
    values = block.astype(jnp.float32)
    mean = jnp.mean(values, axis=1, keepdims=True)
    centred = values - mean
    inv = lax.rsqrt(jnp.mean(centred * centred, axis=1, keepdims=True) + 1e-06)
    return mean, inv


def kernel(
    nr, nc, npower, powers_hbm, expr_hbm, degrees, own_degree,
    powers_ref, expr_ref, left, right, right_mean, right_inv, left_stats, sums_ref, partial, load_sem,
    up_send, down_send, line_recv, plane_send, relay_send, plane_recv, part_send, part_recv, deg_send, deg_recv,
):
    r, c = lax.axis_index("row"), lax.axis_index("col")
    nq = nr // 2
    chip, core = r // 2, r % 2
    twin = r + 1 - 2 * core
    genes, samples = expr_ref.shape
    padded = partial.shape[2]
    rows = genes // HALVES
    genes_all = genes * nr * nc

    def chip_partner(k):
        return (xor(chip, k, nq) if nq & (nq - 1) == 0 else (chip + k) % nq) * 2 + core

    def chip_source(k):
        return (xor(chip, k, nq) if nq & (nq - 1) == 0 else (chip + nq - k) % nq) * 2 + core

    def nth_source(n):
        source, other = chip_source(n // 2), n % 2
        return source + other * (1 - 2 * core)

    loads = (
        pltpu.make_async_copy(expr_hbm, expr_ref, load_sem.at[0]),
        pltpu.make_async_copy(powers_hbm, powers_ref, load_sem.at[1]),
    )
    for load in loads:
        load.start()

    barrier = pltpu.get_barrier_semaphore()

    def greet(row, col):
        pl.semaphore_signal(barrier, inc=1, device_id=(row, col), device_id_type=MESH)

    greet(twin, c)
    for k in range(1, nq):
        greet(chip_partner(k), c)

    @pl.when(c + 1 < nc)
    def _():
        greet(r, c + 1)

    @pl.when(c >= 1)
    def _():
        greet(r, c - 1)

    for load in loads:
        load.wait()

    left[c] = expr_ref[...]
    right[r] = expr_ref[...]
    exponents = [powers_ref[p].astype(jnp.float32) * LOG2E for p in range(npower)]

    def right_stats(index):
        mean, inv = gene_stats(right[index])
        right_mean[index] = jnp.broadcast_to(mean, (genes, 128))
        right_inv[index] = jnp.broadcast_to(inv, (genes, 128))

    pl.semaphore_wait(barrier, nq + jnp.minimum(1, nc - 1 - c) + jnp.minimum(1, c))

    def line_copy(step, half, up):
        block = (c - step) if up else (c + step)
        window = pl.ds(half * rows, rows)
        block = jnp.clip(block, 0, nc - 1)
        target = jnp.clip(c + 1 if up else c - 1, 0, nc - 1)
        source = expr_ref.at[window] if step == 0 else left.at[block, window]
        return pltpu.make_async_remote_copy(
            src_ref=source,
            dst_ref=left.at[block, window],
            send_sem=(up_send if up else down_send).at[step, half],
            recv_sem=line_recv.at[block, half],
            device_id=(r, target),
            device_id_type=MESH,
        )

    def line_sends(step, up):
        return jnp.logical_and(c - step >= 0, c + 1 < nc) if up else jnp.logical_and(c + step < nc, c >= 1)

    def plane_copy(k):
        return pltpu.make_async_remote_copy(
            src_ref=expr_ref, dst_ref=right.at[r],
            send_sem=plane_send.at[k], recv_sem=plane_recv.at[r],
            device_id=(chip_partner(k), c), device_id_type=MESH,
        )

    def relay_copy(k):
        source = chip_source(k) if k else r
        return pltpu.make_async_remote_copy(
            src_ref=right.at[source] if k else expr_ref, dst_ref=right.at[source],
            send_sem=relay_send.at[k], recv_sem=plane_recv.at[source],
            device_id=(twin, c), device_id_type=MESH,
        )

    def plane_arrival(source):
        return pltpu.make_async_remote_copy(
            src_ref=expr_ref, dst_ref=right.at[source],
            send_sem=plane_send.at[0], recv_sem=plane_recv.at[source],
            device_id=(twin, c), device_id_type=MESH,
        )

    def line_arrival(step, half, up):
        block = jnp.clip((c - step) if up else (c + step), 0, nc - 1)
        window = pl.ds(half * rows, rows)
        return pltpu.make_async_remote_copy(
            src_ref=expr_ref.at[window], dst_ref=left.at[block, window],
            send_sem=up_send.at[0, half], recv_sem=line_recv.at[block, half],
            device_id=(r, c), device_id_type=MESH,
        )

    for half in range(HALVES):
        for up in (True, False):
            @pl.when(line_sends(0, up))
            def _():
                line_copy(0, half, up).start()
    for k in range(1, nq):
        plane_copy(k).start()
    relay_copy(0).start()

    def part_copy(d, block):
        return pltpu.make_async_remote_copy(
            src_ref=partial.at[c, block], dst_ref=partial.at[c, block],
            send_sem=part_send.at[d, block], recv_sem=part_recv.at[c, block],
            device_id=(r, (c + d) % nc), device_id_type=MESH,
        )

    def start_left(block):
        mean, inv = gene_stats(left[block])
        left_stats[block, 0] = jnp.broadcast_to(mean, (genes, 128)).T[0:8, :]
        left_stats[block, 1] = jnp.broadcast_to(inv, (genes, 128)).T[0:8, :]

    def run_part(block, first, last):
        if first == last:
            return
        genes_left = left[block]
        mean_row, inv_row = left_stats[block, 0, 0:1, :], left_stats[block, 1, 0:1, :]

        def one_right(turn, sums):
            index = nth_source(turn)
            raw = lax.dot_general(
                right[index], genes_left, (((1,), (1,)), ((), ())), preferred_element_type=jnp.float32
            )
            pearson = (raw * (1.0 / samples) - right_mean[index] * mean_row) * right_inv[index] * inv_row
            log_abs = jnp.log(jnp.abs(pearson))
            return tuple(
                sums[p] + jnp.sum(jnp.exp2(exponents[p] * log_abs).reshape(genes // 8, 8, genes), axis=0)
                for p in range(npower)
            )

        start = tuple(
            sums_ref[block, p] if first else jnp.zeros((8, genes), jnp.float32) for p in range(npower)
        )
        sums = lax.fori_loop(first, last, one_right, start, unroll=2)
        if last < nr:
            for p in range(npower):
                sums_ref[block, p] = sums[p]
            return
        lines = [jnp.sum(total, axis=0, keepdims=True) for total in sums]
        lines.append(jnp.zeros((padded - npower, genes), jnp.float32))
        partial[c, block] = jnp.concatenate(lines, axis=0)

        def send(d, _):
            part_copy(d, block).start()
            return 0

        lax.fori_loop(1, nc, send, 0)

    def both_ways(step, work):
        def one(way, _):
            block = c + step * (2 * way - 1)

            @pl.when(jnp.logical_and(block >= 0, block < nc))
            def _():
                work(block)

            return 0

        lax.fori_loop(0, 2, one, 0)

    def line_step(step, half):
        for up in (True, False):
            @pl.when(c - step >= 0 if up else c + step < nc)
            def _():
                line_arrival(step, half, up).wait_recv()

            if step < nc - 1:
                @pl.when(line_sends(step, up))
                def _():
                    line_copy(step, half, up).start()

    def plane_steps(ks):
        for k in ks:
            plane_arrival(chip_source(k)).wait_recv()
            relay_copy(k).start()
            right_stats(chip_source(k))

    def twin_steps(ks):
        for k in ks:
            source = nth_source(2 * k + 1)
            plane_arrival(source).wait_recv()
            right_stats(source)

    near = list(range(1, max(1, nq - 1)))
    far = list(range(max(1, nq - 1), nq))
    some = 2 * (1 + len(near))
    if some == nr:
        some = 2

    right_stats(r)
    start_left(c)
    twin_steps([0])
    run_part(c, 0, 2)
    for half in range(HALVES):
        line_step(1, half)
    plane_steps(near)
    both_ways(1, start_left)
    if nc > 2:
        line_step(2, 0)
    twin_steps(near)
    run_part(c, 2, some)
    if nc > 2:
        for half in range(1, HALVES):
            line_step(2, half)
    plane_steps(far)
    both_ways(1, lambda block: run_part(block, 0, some))
    twin_steps(far)
    run_part(c, some, nr)
    both_ways(1, lambda block: run_part(block, some, nr))

    def whole(block):
        start_left(block)
        run_part(block, 0, nr)

    for step in range(2, nc):
        if step > 2:
            for half in range(HALVES):
                line_step(step, half)
        both_ways(step, whole)

    def part_wait(d, _):
        source = (c + d) % nc

        def one(block, _):
            pltpu.make_async_remote_copy(
                src_ref=partial.at[c, block], dst_ref=partial.at[source, block],
                send_sem=part_send.at[d, block], recv_sem=part_recv.at[source, block],
                device_id=(r, source), device_id_type=MESH,
            ).wait_recv()
            return 0

        return lax.fori_loop(0, nc, one, 0)

    lax.fori_loop(1, nc, part_wait, 0)
    lines = []
    for block in range(nc):
        total = partial[0, block]
        for source in range(1, nc):
            total = total + partial[source, block]
        lines.append(total[:npower])
    spare = degrees.shape[1] - nc * npower
    if spare:
        lines.append(jnp.zeros((spare, genes), jnp.float32))
    degrees[r] = jnp.concatenate(lines, axis=0)

    def deg_copy(d):
        return pltpu.make_async_remote_copy(
            src_ref=degrees.at[r], dst_ref=degrees.at[r],
            send_sem=deg_send.at[d], recv_sem=deg_recv.at[r],
            device_id=((r + d) % nr, c), device_id_type=MESH,
        )

    def deg_start(d, _):
        deg_copy(d).start()
        return 0

    def deg_wait(d, _):
        source = (r + d) % nr
        pltpu.make_async_remote_copy(
            src_ref=degrees.at[r], dst_ref=degrees.at[source],
            send_sem=deg_send.at[d], recv_sem=deg_recv.at[source],
            device_id=(source, c), device_id_type=MESH,
        ).wait_recv()
        return 0

    lax.fori_loop(1, nr, deg_start, 0)
    own = partial[0, c]
    for source in range(1, nc):
        own = own + partial[source, c]
    own_degree[...] = own

    for half in range(HALVES):
        for up in (True, False):
            for step in range(nc - 1):
                @pl.when(line_sends(step, up))
                def _():
                    line_copy(step, half, up).wait_send()
    for k in range(1, nq):
        plane_copy(k).wait_send()
    for k in range(nq):
        relay_copy(k).wait_send()

    def part_done(d, _):
        def one(block, _):
            part_copy(d, block).wait_send()
            return 0

        return lax.fori_loop(0, nc, one, 0)

    lax.fori_loop(1, nc, part_done, 0)
    lax.fori_loop(1, nr, deg_wait, 0)

    lax.fori_loop(1, nr, lambda d, _: (deg_copy(d).wait_send(), 0)[1], 0)


def fit_kernel(nr, nc, npower, degrees, own_degree, log_degree_ref, freq_ref, slope_ref, mean_log_ref):
    height, genes = degrees.shape[1:]
    padded = own_degree.shape[0]
    genes_all = genes * nr * nc
    spare = height - nc * npower
    log_degree_ref[...] = (jnp.log(own_degree[...]) * LOG10E)[:npower]

    def fold(values, combine):
        total = values[:npower]
        for block in range(1, nc):
            total = combine(total, values[block * npower:(block + 1) * npower])
        return jnp.concatenate([total, jnp.ones((padded - npower, 1), jnp.float32)], axis=0)

    best = lax.fori_loop(1, nr, lambda index, best: jnp.maximum(best, degrees[index]), degrees[0])
    peak = fold(jnp.max(best, axis=1, keepdims=True), jnp.maximum)
    scales = [(BINS / peak)[:npower]] * nc
    if spare:
        scales.append(jnp.ones((spare, 1), jnp.float32))
    scale = jnp.broadcast_to(jnp.concatenate(scales, axis=0), (height, genes))

    def weigh(index, carry):
        carry = list(carry)
        degree = degrees[index]
        position = jnp.clip(degree * scale - 0.5, 0.0, BINS - 1.0)
        for b in range(BINS):
            carry[b] = carry[b] + jnp.maximum(0.0, 1.0 - jnp.abs(position - b))
        carry[BINS] = carry[BINS] + degree
        return tuple(carry)

    totals = lax.fori_loop(0, nr, weigh, tuple(jnp.zeros((height, genes), jnp.float32) for _ in range(BINS + 1)))
    totals = [fold(jnp.sum(total, axis=1, keepdims=True), jnp.add) for total in totals]
    lane = lax.broadcasted_iota(jnp.int32, (padded, 128), 1)
    line = lax.broadcasted_iota(jnp.int32, (padded, 128), 0)
    freq = jnp.zeros((padded, 128), jnp.float32)
    for b in range(BINS):
        freq = jnp.where(lane == b, totals[b], freq)
    freq = freq / genes_all
    freq_ref[...] = freq[:npower, :BINS]
    mean_log = jnp.log(totals[BINS] / genes_all) * LOG10E
    inside = lane < BINS
    xfit = jnp.log((lane.astype(jnp.float32) + 0.5) * peak / BINS) * LOG10E
    yfit = jnp.log(freq + 1.0 / genes_all) * LOG10E

    def deviation(values):
        mean = jnp.sum(jnp.where(inside, values, 0.0), axis=1, keepdims=True) / BINS
        return jnp.where(inside, values - mean, 0.0)

    xdev, ydev = deviation(xfit), deviation(yfit)
    slope = jnp.sum(xdev * ydev, axis=1, keepdims=True) / jnp.sum(xdev * xdev, axis=1, keepdims=True)
    on_line = jnp.logical_and(lane == line, line < npower)
    slope_ref[...] = jnp.sum(jnp.where(on_line, slope, 0.0), axis=0, keepdims=True)[:, :npower]
    mean_log_ref[...] = jnp.sum(jnp.where(on_line, mean_log, 0.0), axis=0, keepdims=True)[:, :npower]


def solution(mesh):
    nr, nc = mesh.shape["row"], mesh.shape["col"]

    def on_device(expression, powers):
        genes, samples = expression.shape
        npower = powers.shape[0]
        padded = -(-npower // 8) * 8
        if padded == npower:
            padded += 8
        height = -(-npower * nc // 8) * 8
        vmem = pl.BlockSpec(memory_space=pltpu.VMEM)
        hbm = pl.BlockSpec(memory_space=pltpu.HBM)
        dma = pltpu.SemaphoreType.DMA
        degrees, own_degree = pl.pallas_call(
            functools.partial(kernel, nr, nc, npower),
            out_shape=(
                jax.ShapeDtypeStruct((nr, height, genes), jnp.float32),
                jax.ShapeDtypeStruct((padded, genes), jnp.float32),
            ),
            in_specs=[hbm, hbm],
            out_specs=(vmem, vmem),
            scratch_shapes=[
                pltpu.SMEM((npower,), jnp.int32),
                pltpu.VMEM((genes, samples), jnp.bfloat16),
                pltpu.VMEM((nc, genes, samples), jnp.bfloat16),
                pltpu.VMEM((nr, genes, samples), jnp.bfloat16),
                pltpu.VMEM((nr, genes, 128), jnp.float32),
                pltpu.VMEM((nr, genes, 128), jnp.float32),
                pltpu.VMEM((nc, 2, 8, genes), jnp.float32),
                pltpu.VMEM((nc, npower, 8, genes), jnp.float32),
                pltpu.VMEM((nc, nc, padded, genes), jnp.float32),
                dma((2,)),
                dma((nc, HALVES)),
                dma((nc, HALVES)),
                dma((nc, HALVES)),
                dma((nr // 2,)),
                dma((nr // 2,)),
                dma((nr,)),
                dma((nc, nc)),
                dma((nc, nc)),
                dma((nr,)),
                dma((nr,)),
            ],
            compiler_params=pltpu.CompilerParams(
                collective_id=0, has_side_effects=True, vmem_limit_bytes=67043328
            ),
        )(powers, expression)
        log_degree, freq, slope, mean_log = pl.pallas_call(
            functools.partial(fit_kernel, nr, nc, npower),
            out_shape=(
                jax.ShapeDtypeStruct((npower, genes), jnp.float32),
                jax.ShapeDtypeStruct((npower, BINS), jnp.float32),
                jax.ShapeDtypeStruct((1, npower), jnp.float32),
                jax.ShapeDtypeStruct((1, npower), jnp.float32),
            ),
            in_specs=[vmem, vmem],
            out_specs=(vmem,) * 4,
        )(degrees, own_degree)
        return log_degree, freq, slope.reshape(npower), mean_log.reshape(npower)

    return jax.shard_map(
        on_device,
        mesh=mesh,
        in_specs=(P(("row", "col"), None), P()),
        out_specs=(P(None, ("row", "col")), P(), P(), P()),
        check_vma=False,
    )
```

profile of v0, /device:TPU:0, one launch (start us, length us, event | category | flops | bytes accessed | tf_op | source)
XLA Modules:
  0.0 37.7 jit_solution(3829636109478419388)
XLA Ops:
  0.6 34.6 %shard_map.57 = (f32[8,40,128]{2,1,0:T(8,128)}, f32[16,128]{1,0:T(8,128)}) custom-call(s32[10]{0:T(128)} %powers_hbm.1, bf16[128,1024]{1,0:T(8,128)(2,1)} %expr_hbm.1), custom_call_target="tpu_custom_call" | custom-call | tf_op jit(solution)/shard_map/pallas_call | solution.py:417
  35.3 2.4 %shard_map.58 = (f32[10,128]{1,0:T(8,128)}, f32[10,10]{1,0:T(8,128)}, f32[1,10]{1,0:T(1,128)}, f32[1,10]{1,0:T(1,128)}) custom-call(f32[8,40,128]{2,1,0:T(8,128)} %get-tuple-element.10.degrees, f32[16,128]{1,0:T(8,128)} %get-tuple-element.11.own_degree), custom_call_target="tpu_custom_call" | custom-call | tf_op jit(solution)/shard_map/pallas_call | solution.py:451
where the time goes:
time: 37.8 us; the launch traced here: 37.7 us
  Pallas kernels  37.1 us (98%)
  between operations  0.64 us (2%)
    pallas_call x1, Pallas kernels, on_device(): pl.pallas_call(functools.partial(kernel, nr, nc, npower), out_shape=(jax....  34.6 us
    pallas_call x1, Pallas kernels, on_device(): pl.pallas_call(functools.partial(fit_kernel, nr, nc, npower), out_shape=(...  2.44 us

commit v1 on v0

v1 whole, which is shorter than its diff:
```python
import functools
import math

import jax
import jax.numpy as jnp
from jax import lax
from jax.experimental import pallas as pl
from jax.experimental.pallas import tpu as pltpu
from jax.sharding import PartitionSpec as P

BINS = 10
EDGES = (0, 2, 4, 6, 7, 8)
CHUNKS = len(EDGES) - 1
LATE = 3
STATS = CHUNKS
STRIP = 32
LOG2E = math.log2(math.e)
LOG10E = math.log10(math.e)
MESH = pl.DeviceIdType.MESH


def split(size):
    low = max(f for f in range(1, math.isqrt(size) + 1) if size % f == 0)
    return size // low, low


def kernel(
    n0, n1, nh, nl, npower, powers_hbm, expr_hbm, log_degree_ref, fit_ref,
    powers_ref, left, right, stats, right_mean, right_inv, raw_ref, sums_ref, partial, degrees,
    load_sem, far_send, side_send, near_send, up_send, twin_send, stat_send,
    far_recv, side_recv, near_recv, up_recv, twin_recv, stat_recv, part_sem, deg_sem,
):
    r, c = lax.axis_index("row"), lax.axis_index("col")
    q, core = r // 2, r % 2
    q1, q0 = q // n0, q % n0
    ch, cl = c // nl, c % nl
    nleft, npair = nh * n0, nl * n1
    _, genes, samples = left.shape
    edges = [genes * e // EDGES[-1] for e in EDGES]
    late = 2 * edges[LATE]

    def device(d0=0, dh=0, d1=0, dl=0, other=False):
        row = (((q1 + d1) % n1) * n0 + (q0 + d0) % n0) * 2 + (1 - core if other else core)
        return row, ((ch + dh) % nh) * nl + (cl + dl) % nl

    def left_slot(dh, d0):
        return ((ch + nh - dh) % nh) * n0 + (q0 + n0 - d0) % n0

    def pair_slot(dl, d1):
        return ((cl + nl - dl) % nl) * n1 + (q1 + n1 - d1) % n1

    own_left, own_pair = left_slot(0, 0), pair_slot(0, 0)
    block = left.at[own_left]

    def left_piece(slot, k):
        if k == STATS:
            return stats.at[slot]
        return left.at[slot, pl.ds(edges[k], edges[k + 1] - edges[k])]

    def right_piece(slot, side, k):
        if k == STATS:
            return stats.at[nleft + slot * 2 + side]
        size = edges[k + 1] - edges[k]
        return right.at[slot, pl.ds(2 * edges[k] + side * size, size)]

    loads = [
        pltpu.make_async_copy(expr_hbm, block, load_sem.at[0]),
        pltpu.make_async_copy(powers_hbm, powers_ref, load_sem.at[1]),
    ]
    for load in loads:
        load.start()
    for k in range(CHUNKS):
        source = expr_hbm.at[pl.ds(edges[k], edges[k + 1] - edges[k])]
        pltpu.make_async_copy(source, right_piece(own_pair, core, k), load_sem.at[2]).start()

    barrier = pltpu.get_barrier_semaphore()
    greeted = [dict(other=True)]
    greeted += [dict(d0=d) for d in range(1, n0)]
    greeted += [dict(d1=d) for d in range(1, n1)]
    greeted += [dict(dh=d) for d in range(1, nh)]
    greeted += [dict(dl=d) for d in range(1, nl)]
    for where in greeted:
        pl.semaphore_signal(barrier, inc=1, device_id=device(**where), device_id_type=MESH)

    loads.append(pltpu.make_async_copy(expr_hbm, block, load_sem.at[2]))
    for load in loads:
        load.wait()

    values = left[own_left].astype(jnp.float32)
    mean = jnp.mean(values, axis=1, keepdims=True)
    centred = values - mean
    inv = lax.rsqrt(jnp.mean(centred * centred, axis=1, keepdims=True) + 1e-06)
    own_stats = jnp.concatenate(
        [jnp.broadcast_to(mean, (genes, 128)).T[0:1, :], jnp.broadcast_to(inv, (genes, 128)).T[0:1, :]], axis=0
    )
    stats[own_left] = own_stats
    stats[nleft + own_pair * 2 + core] = own_stats
    for slot in range(nleft):
        for p in range(npower):
            sums_ref[slot, p] = jnp.zeros((8, genes), jnp.float32)
    exponents = [powers_ref[p].astype(jnp.float32) * LOG2E for p in range(npower)]

    pl.semaphore_wait(barrier, len(greeted))

    def remote(ref, send, recv, where):
        return pltpu.make_async_remote_copy(
            src_ref=ref, dst_ref=ref, send_sem=send, recv_sem=recv, device_id=device(**where), device_id_type=MESH
        )

    flows = [("far", dh, 0) for dh in range(1, nh)] + [("near", dl, 0) for dl in range(1, nl)]
    flows += [("side", dh, d0) for dh in range(nh) for d0 in range(1, n0)]
    flows += [("up", dl, d1) for dl in range(nl) for d1 in range(1, n1)]
    flows += [("twin", dl, d1) for dl in range(nl) for d1 in range(n1)]

    def sems(kind, a, b, k):
        if k == STATS:
            return stat_send.at[0], stat_recv.at[flows.index((kind, a, b))]
        if kind == "far":
            return far_send.at[a - 1], far_recv.at[a - 1, k]
        if kind == "near":
            return near_send.at[a - 1], near_recv.at[a - 1, k]
        if kind == "side":
            return side_send.at[a, b - 1], side_recv.at[a, b - 1]
        if kind == "up":
            return up_send.at[a, b - 1], up_recv.at[a, b - 1, k]
        return twin_send.at[a, b], twin_recv.at[a, b, int(k >= LATE)]

    def send(kind, a, b, k):
        if kind == "far":
            ref, where = left_piece(own_left, k), dict(dh=a)
        elif kind == "side":
            ref, where = left_piece(left_slot(a, 0), k), dict(d0=b)
        elif kind == "near":
            ref, where = right_piece(own_pair, core, k), dict(dl=a)
        elif kind == "up":
            ref, where = right_piece(pair_slot(a, 0), core, k), dict(d1=b)
        else:
            ref, where = right_piece(pair_slot(a, b), core, k), dict(other=True)
        remote(ref, *sems(kind, a, b, k), where).start()

    def wait(kind, a, b, k, ref):
        remote(ref, *sems(kind, a, b, k), dict(other=True)).wait_recv()

    def wait_far(dh, k):
        wait("far", dh, 0, k, left_piece(left_slot(dh, 0), k))

    def wait_side(dh, d0, k):
        wait("side", dh, d0, k, left_piece(left_slot(dh, d0), k) if k == STATS else left.at[left_slot(dh, d0)])

    def wait_near(dl, k):
        wait("near", dl, 0, k, right_piece(pair_slot(dl, 0), core, k))

    def wait_up(dl, d1, k):
        wait("up", dl, d1, k, right_piece(pair_slot(dl, d1), core, k))

    def wait_twin(dl, d1, k):
        slot = pair_slot(dl, d1)
        if k == STATS:
            ref = right_piece(slot, 1 - core, k)
        else:
            ref = right.at[slot, pl.ds(0, edges[LATE]) if k < LATE else pl.ds(late, genes - edges[LATE])]
        wait("twin", dl, d1, k, ref)

    for k in (STATS, *range(CHUNKS)):
        for first in (0, 1):
            @pl.when(core == first)
            def _():
                for kind in ("far", "near") if first == 0 else ("near", "far"):
                    for a in range(1, nh if kind == "far" else nl):
                        send(kind, a, 0, k)

        for d0 in range(1, n0):
            send("side", 0, d0, k)
        for d1 in range(1, n1):
            send("up", 0, d1, k)
        send("twin", 0, 0, k)

    def multiply(ls, blocks, ps, pairs, lo=0, hi=2 * genes):
        size = hi - lo
        lhs = right[pl.ds(ps, pairs), lo:hi].reshape(pairs * size, samples)
        rhs = left[pl.ds(ls, blocks)].reshape(blocks * genes, samples)
        raw = lax.dot_general(lhs, rhs, (((1,), (1,)), ((), ())), preferred_element_type=jnp.float32)
        for a in range(blocks):
            for b in range(pairs):
                raw_ref[ls + a, ps + b, lo:hi] = raw[b * size:(b + 1) * size, a * genes:(a + 1) * genes]

    def accumulate(ls, ps, lo=0, hi=2 * genes):
        mean_row, inv_row = stats[ls, 0:1, :], stats[ls, 1:2, :]
        totals = [None] * npower
        for s in range(lo, hi, STRIP):
            raw = raw_ref[ls, ps, s:s + STRIP, :]
            mean_col, inv_col = right_mean[ps, s:s + STRIP, :], right_inv[ps, s:s + STRIP, :]
            pearson = (raw * (1.0 / samples) - mean_col * mean_row) * inv_col * inv_row
            log_abs = jnp.log(jnp.abs(pearson))
            for p in range(npower):
                part = jnp.sum(jnp.exp2(exponents[p] * log_abs).reshape(STRIP // 8, 8, genes), axis=0)
                totals[p] = part if totals[p] is None else totals[p] + part
        for p in range(npower):
            sums_ref[ls, p] = sums_ref[ls, p] + totals[p]

    def run(ls, blocks, ps, pairs, lo=0, hi=2 * genes):
        multiply(ls, blocks, ps, pairs, lo, hi)

        def body(u, _):
            accumulate(ls + lax.rem(u, blocks), ps + lax.div(u, blocks), lo, hi)
            return 0

        lax.fori_loop(0, blocks * pairs, body, 0)

    def columns(dl, d1):
        slot = pair_slot(dl, d1)
        for side in (0, 1):
            row = stats[nleft + slot * 2 + side]
            mean_col = jnp.broadcast_to(row[0:1], (128, genes)).T
            inv_col = jnp.broadcast_to(row[1:2], (128, genes)).T
            for k in range(CHUNKS):
                low, high = edges[k], edges[k + 1]
                window = pl.ds(2 * low + side * (high - low), high - low)
                right_mean[slot, window] = mean_col[low:high]
                right_inv[slot, window] = inv_col[low:high]

    own_row, own_line = ch * n0, cl * n1
    far_pairs = [(dl, 0) for dl in range(1, nl)]
    rest_pairs = [(dl, d1) for dl in range(1, nl) for d1 in range(1, n1)]
    far_rows = [(ch + nh - dh) % nh * n0 for dh in range(1, nh)]
    far_blocks = [left_slot(dh, 0) for dh in range(1, nh)]
    rest_blocks = [(dh, d0) for dh in range(1, nh) for d0 in range(1, n0)]

    def pass_up(k):
        for d1 in range(1, n1):
            wait_up(0, d1, k)
            send("twin", 0, d1, k)

    def pass_far(k):
        for dl in range(1, nl):
            wait_near(dl, k)
            for d1 in range(1, n1):
                send("up", dl, d1, k)
            send("twin", dl, 0, k)
        for dh in range(1, nh):
            wait_far(dh, k)
            for d0 in range(1, n0):
                send("side", dh, d0, k)

    def pass_rest(k):
        for dl, d1 in rest_pairs:
            wait_up(dl, d1, k)
            send("twin", dl, d1, k)

    wait_twin(0, 0, STATS)
    wait_twin(0, 0, 0)
    wait_twin(0, 0, LATE)
    columns(0, 0)
    pass_up(STATS)
    pass_far(STATS)
    pass_up(0)
    pass_up(1)
    pass_far(0)
    pass_rest(STATS)
    pass_up(2)
    pass_up(3)
    for dl in range(nl):
        for d1 in range(n1):
            if dl or d1:
                wait_twin(dl, d1, STATS)
                columns(dl, d1)
    for dh in range(nh):
        for d0 in range(1, n0):
            wait_side(dh, d0, STATS)
    pass_up(4)
    pass_far(1)
    for d0 in range(1, n0):
        wait_side(0, d0, 0)
    run(own_row, n0, own_pair, 1)
    pass_rest(0)
    for d1 in range(1, n1):
        wait_twin(0, d1, 0)
        wait_twin(0, d1, LATE)
        run(own_row, n0, pair_slot(0, d1), 1)
    pass_far(2)
    pass_rest(1)
    pass_far(3)
    for dl, d1 in far_pairs:
        wait_twin(dl, d1, 0)
        run(own_row, n0, pair_slot(dl, d1), 1, 0, late)
    pass_far(4)
    for b in far_blocks:
        run(b, 1, own_line, n1)
    pass_rest(2)
    for dl, d1 in far_pairs:
        wait_twin(dl, d1, LATE)
        for b in far_blocks:
            run(b, 1, pair_slot(dl, d1), 1)
        run(own_row, n0, pair_slot(dl, d1), 1, late)
    pass_rest(3)
    pass_rest(4)
    for dh, d0 in rest_blocks:
        wait_side(dh, d0, 0)
        run(left_slot(dh, d0), 1, own_line, n1)
        for m in far_pairs:
            run(left_slot(dh, d0), 1, pair_slot(*m), 1)
    for dl, d1 in rest_pairs:
        wait_twin(dl, d1, 0)
        wait_twin(dl, d1, LATE)
        run(0, nleft, pair_slot(dl, d1), 1)

    height = partial.shape[1]
    lines = [
        jnp.sum(sums_ref[slot, p], axis=0, keepdims=True) for slot in range(nleft) for p in range(npower)
    ]
    if height > nleft * npower:
        lines.append(jnp.zeros((height - nleft * npower, genes), jnp.float32))
    partial[own_left] = jnp.concatenate(lines, axis=0)

    mine_part = partial.at[own_left]
    for dh in reversed(range(nh)):
        for d0 in reversed(range(n0)):
            if dh or d0:
                remote(mine_part, part_sem.at[0], part_sem.at[1], dict(dh=dh, d0=d0)).start()
    others = partial.at[pl.ds(0, nleft - 1)]
    remote(others, part_sem.at[0], part_sem.at[1], dict(other=True)).wait_recv()
    total = partial[0]
    for slot in range(1, nleft):
        total = total + partial[slot]
    own = own_pair * 2 + core
    degrees[own] = total

    for dl in reversed(range(nl)):
        for d1 in reversed(range(n1)):
            for o in (True, False):
                if dl or d1 or o:
                    remote(degrees.at[own], deg_sem.at[0], deg_sem.at[1], dict(dl=dl, d1=d1, other=o)).start()
    mine = total[:npower]
    for slot in range(1, nleft):
        mine = jnp.where(own_left == slot, total[slot * npower:(slot + 1) * npower], mine)
    log_degree_ref[...] = jnp.log(mine) * LOG10E

    for kind, a, b in flows:
        remote(block, *sems(kind, a, b, 0), dict(other=True)).wait_send()
    remote(stats.at[pl.ds(0, len(flows))], *sems(*flows[0], STATS), dict(other=True)).wait_send()
    remote(others, part_sem.at[0], part_sem.at[1], dict(other=True)).wait_send()
    rest = degrees.at[pl.ds(0, 2 * npair - 1)]
    remote(rest, deg_sem.at[0], deg_sem.at[1], dict(other=True)).wait_recv()
    fit(genes * nleft * npair * 2, nleft, npower, degrees, fit_ref)
    remote(rest, deg_sem.at[0], deg_sem.at[1], dict(other=True)).wait_send()


def fit(genes_all, nleft, npower, degrees, fit_ref):
    blocks, height, genes = degrees.shape
    padded = npower + 8 - npower % 8
    spare = height - nleft * npower

    def fold(values, combine):
        total = values[:npower]
        for block in range(1, nleft):
            total = combine(total, values[block * npower:(block + 1) * npower])
        return jnp.concatenate([total, jnp.ones((padded - npower, 1), jnp.float32)], axis=0)

    best = lax.fori_loop(1, blocks, lambda index, best: jnp.maximum(best, degrees[index]), degrees[0])
    peak = fold(jnp.max(best, axis=1, keepdims=True), jnp.maximum)
    scales = [(BINS / peak)[:npower]] * nleft
    if spare:
        scales.append(jnp.ones((spare, 1), jnp.float32))
    scale = jnp.broadcast_to(jnp.concatenate(scales, axis=0), (height, genes))

    def weigh(index, carry):
        carry = list(carry)
        degree = degrees[index]
        position = jnp.clip(degree * scale - 0.5, 0.0, BINS - 1.0)
        for b in range(BINS):
            carry[b] = carry[b] + jnp.maximum(0.0, 1.0 - jnp.abs(position - b))
        carry[BINS] = carry[BINS] + degree
        return tuple(carry)

    totals = lax.fori_loop(0, blocks, weigh, tuple(jnp.zeros((height, genes), jnp.float32) for _ in range(BINS + 1)))
    totals = [fold(jnp.sum(total, axis=1, keepdims=True), jnp.add) for total in totals]
    lane = lax.broadcasted_iota(jnp.int32, (padded, 128), 1)
    line = lax.broadcasted_iota(jnp.int32, (padded, 128), 0)
    freq = jnp.zeros((padded, 128), jnp.float32)
    for b in range(BINS):
        freq = jnp.where(lane == b, totals[b], freq)
    freq = freq / genes_all
    fit_ref[0:padded, :] = freq
    mean_log = jnp.log(totals[BINS] / genes_all) * LOG10E
    inside = lane < BINS
    xfit = jnp.log((lane.astype(jnp.float32) + 0.5) * peak / BINS) * LOG10E
    yfit = jnp.log(freq + 1.0 / genes_all) * LOG10E

    def deviation(values):
        mean = jnp.sum(jnp.where(inside, values, 0.0), axis=1, keepdims=True) / BINS
        return jnp.where(inside, values - mean, 0.0)

    xdev, ydev = deviation(xfit), deviation(yfit)
    slope = jnp.sum(xdev * ydev, axis=1, keepdims=True) / jnp.sum(xdev * xdev, axis=1, keepdims=True)
    on_line = jnp.logical_and(lane == line, line < npower)
    fit_ref[padded:padded + 1, :] = jnp.sum(jnp.where(on_line, slope, 0.0), axis=0, keepdims=True)
    fit_ref[padded + 1:padded + 2, :] = jnp.sum(jnp.where(on_line, mean_log, 0.0), axis=0, keepdims=True)


def unpack_kernel(npower, log_degree_in, fit_in, log_degree_ref, freq_ref, slope_ref, mean_log_ref):
    padded = fit_in.shape[0] - 8
    log_degree_ref[...] = log_degree_in[...]
    freq_ref[...] = fit_in[0:npower, :BINS]
    slope_ref[...] = fit_in[padded:padded + 1, :npower]
    mean_log_ref[...] = fit_in[padded + 1:padded + 2, :npower]


def solution(mesh):
    nr, nc = mesh.shape["row"], mesh.shape["col"]
    n1, n0 = split(nr // 2)
    nh, nl = split(nc)

    def on_device(expression, powers):
        genes, samples = expression.shape
        npower = powers.shape[0]
        nleft, npair = nh * n0, nl * n1
        height = -(-npower * nleft // 8) * 8
        vmem = pl.BlockSpec(memory_space=pltpu.VMEM)
        hbm = pl.BlockSpec(memory_space=pltpu.HBM)
        dma = pltpu.SemaphoreType.DMA
        f32 = jnp.float32
        padded = npower + 8 - npower % 8
        log_degree, packed = pl.pallas_call(
            functools.partial(kernel, n0, n1, nh, nl, npower),
            out_shape=(
                jax.ShapeDtypeStruct((npower, genes), f32),
                jax.ShapeDtypeStruct((padded + 8, 128), f32),
            ),
            in_specs=[hbm, hbm],
            out_specs=(vmem, vmem),
            scratch_shapes=[
                pltpu.SMEM((npower,), jnp.int32),
                pltpu.VMEM((nleft, genes, samples), jnp.bfloat16),
                pltpu.VMEM((npair, 2 * genes, samples), jnp.bfloat16),
                pltpu.VMEM((nleft + 2 * npair, 2, genes), f32),
                pltpu.VMEM((npair, 2 * genes, 128), f32),
                pltpu.VMEM((npair, 2 * genes, 128), f32),
                pltpu.VMEM((nleft, npair, 2 * genes, genes), f32),
                pltpu.VMEM((nleft, npower, 8, genes), f32),
                pltpu.VMEM((nleft, height, genes), f32),
                pltpu.VMEM((2 * npair, height, genes), f32),
                dma((3,)),
                dma((nh - 1,)),
                dma((nh, n0 - 1)),
                dma((nl - 1,)),
                dma((nl, n1 - 1)),
                dma((nl, n1)),
                dma((1,)),
                dma((nh - 1, CHUNKS)),
                dma((nh, n0 - 1)),
                dma((nl - 1, CHUNKS)),
                dma((nl, n1 - 1, CHUNKS)),
                dma((nl, n1, 2)),
                dma((nleft + 2 * npair - 2,)),
                dma((2,)),
                dma((2,)),
            ],
            compiler_params=pltpu.CompilerParams(
                collective_id=0, has_side_effects=True, vmem_limit_bytes=67043328
            ),
        )(powers, expression)
        log_degree, freq, slope, mean_log = pl.pallas_call(
            functools.partial(unpack_kernel, npower),
            out_shape=(
                jax.ShapeDtypeStruct((npower, genes), f32),
                jax.ShapeDtypeStruct((npower, BINS), f32),
                jax.ShapeDtypeStruct((1, npower), f32),
                jax.ShapeDtypeStruct((1, npower), f32),
            ),
            in_specs=[vmem, vmem],
            out_specs=(vmem,) * 4,
        )(log_degree, packed)
        return log_degree, freq, slope.reshape(npower), mean_log.reshape(npower)

    return jax.shard_map(
        on_device,
        mesh=mesh,
        in_specs=(P(("row", "col"), None), P()),
        out_specs=(P(None, ("row", "col")), P(), P(), P()),
        check_vma=False,
    )
```

time: 37.8 us -> 36.7 us (0.971)
  Pallas kernels: 37.1 us -> 35.8 us
    pallas_call x2, Pallas kernels: 37.1 us -> 35.8 us  [the longest x1 34.5 us: on_device(): pl.pallas_call(functools.partial(kernel, n0, n1, nh, nl, npower), out_sha...]
where the time goes in v1:
time: 36.7 us; the launch traced here: 36.4 us
  Pallas kernels  35.8 us (98%)
  between operations  0.64 us (2%)
    pallas_call x1, Pallas kernels, on_device(): pl.pallas_call(functools.partial(kernel, n0, n1, nh, nl, npower), out_sha...  34.5 us
    pallas_call x1, Pallas kernels, on_device(): pl.pallas_call(functools.partial(unpack_kernel, npower), out_shape=(jax.S...  1.33 us

profile of v1, /device:TPU:0, one launch (start us, length us, event | category | flops | bytes accessed | tf_op | source)
XLA Modules:
  0.0 36.4 jit_solution(4724776728668377429)
XLA Ops:
  0.6 34.5 %shard_map.57 = (f32[10,128]{1,0:T(8,128)}, f32[24,128]{1,0:T(8,128)}) custom-call(s32[10]{0:T(128)} %powers_hbm.1, bf16[128,1024]{1,0:T(8,128)(2,1)} %expr_hbm.1), custom_call_target="tpu_custom_call" | custom-call | tf_op jit(solution)/shard_map/pallas_call | solution.py:423
  35.1 1.3 %shard_map.58 = (f32[10,128]{1,0:T(8,128)}, f32[10,10]{1,0:T(8,128)}, f32[1,10]{1,0:T(1,128)}, f32[1,10]{1,0:T(1,128)}) custom-call(f32[10,128]{1,0:T(8,128)} %get-tuple-element.10.log_degree_in, f32[24,128]{1,0:T(8,128)} %get-tuple-element.11.fit_in), custom_call_target="tpu_custom_call" | custom-call | tf_op jit(solution)/shard_map/pallas_call | solution.py:462

commit v2 on v1

--- a/solution.py
+++ b/solution.py
@@ -11,7 +11,7 @@
 BINS = 10
 EDGES = (0, 2, 4, 6, 7, 8)
 CHUNKS = len(EDGES) - 1
-LATE = 3
+LATE = 2
 STATS = CHUNKS
 STRIP = 32
 LOG2E = math.log2(math.e)
@@ -27,7 +27,7 @@
 def kernel(
     n0, n1, nh, nl, npower, powers_hbm, expr_hbm, log_degree_ref, fit_ref,
     powers_ref, left, right, stats, right_mean, right_inv, raw_ref, sums_ref, partial, degrees,
-    load_sem, far_send, side_send, near_send, up_send, twin_send, stat_send,
+    load_sem, send_sem,
     far_recv, side_recv, near_recv, up_recv, twin_recv, stat_recv, part_sem, deg_sem,
 ):
     r, c = lax.axis_index("row"), lax.axis_index("col")
@@ -114,16 +114,16 @@
 
     def sems(kind, a, b, k):
         if k == STATS:
-            return stat_send.at[0], stat_recv.at[flows.index((kind, a, b))]
+            return send_sem.at[0], stat_recv.at[flows.index((kind, a, b))]
         if kind == "far":
-            return far_send.at[a - 1], far_recv.at[a - 1, k]
+            return send_sem.at[1], far_recv.at[a - 1, k]
         if kind == "near":
-            return near_send.at[a - 1], near_recv.at[a - 1, k]
+            return send_sem.at[1], near_recv.at[a - 1, k]
         if kind == "side":
-            return side_send.at[a, b - 1], side_recv.at[a, b - 1]
+            return send_sem.at[1], side_recv.at[a, b - 1]
         if kind == "up":
-            return up_send.at[a, b - 1], up_recv.at[a, b - 1, k]
-        return twin_send.at[a, b], twin_recv.at[a, b, int(k >= LATE)]
+            return send_sem.at[2], up_recv.at[a, b - 1, k]
+        return send_sem.at[2], twin_recv.at[a, b, int(k >= LATE)]
 
     def send(kind, a, b, k):
         if kind == "far":
@@ -198,9 +198,16 @@
         for p in range(npower):
             sums_ref[ls, p] = sums_ref[ls, p] + totals[p]
 
-    def run(ls, blocks, ps, pairs, lo=0, hi=2 * genes):
-        multiply(ls, blocks, ps, pairs, lo, hi)
-
+    def part(ls, blocks, ps, pairs, lo=0, hi=2 * genes):
+        return ls, blocks, ps, pairs, lo, hi
+
+    def run(*parts):
+        for each in parts:
+            multiply(*each)
+        for each in parts:
+            add(*each)
+
+    def add(ls, blocks, ps, pairs, lo=0, hi=2 * genes):
         def body(u, _):
             accumulate(ls + lax.rem(u, blocks), ps + lax.div(u, blocks), lo, hi)
             return 0
@@ -225,6 +232,28 @@
     far_rows = [(ch + nh - dh) % nh * n0 for dh in range(1, nh)]
     far_blocks = [left_slot(dh, 0) for dh in range(1, nh)]
     rest_blocks = [(dh, d0) for dh in range(1, nh) for d0 in range(1, n0)]
+
+    early_blocks = [(0, d0) for d0 in range(n0)]
+    late_blocks = [(dh, d0) for dh in range(1, nh) for d0 in range(n0)]
+    far_lines = [(cl + nl - dl) % nl * n1 for dl in range(1, nl)]
+
+    def index_of(a, b, dh, d0):
+        return (a * n0 + b) * nleft + dh * n0 + d0
+
+    def send_partials(group):
+        for m in group:
+            slot = left_slot(*m)
+            rows = [jnp.sum(sums_ref[slot, p], axis=0, keepdims=True) for p in range(npower)]
+            partial[index_of(0, 0, *m)] = jnp.concatenate(rows, axis=0)
+        for a in reversed(range(nh)):
+            for b in reversed(range(n0)):
+                for m in group:
+                    if a or b:
+                        pltpu.make_async_remote_copy(
+                            src_ref=partial.at[index_of(0, 0, *m)], dst_ref=partial.at[index_of(a, b, *m)],
+                            send_sem=part_sem.at[0], recv_sem=part_sem.at[1 if group is early_blocks else 2],
+                            device_id=device(dh=a, d0=b), device_id_type=MESH,
+                        ).start()
 
     def pass_up(k):
         for d1 in range(1, n1):
@@ -271,57 +300,69 @@
     pass_far(1)
     for d0 in range(1, n0):
         wait_side(0, d0, 0)
-    run(own_row, n0, own_pair, 1)
+    run(part(own_row, n0, own_pair, 1))
     pass_rest(0)
     for d1 in range(1, n1):
         wait_twin(0, d1, 0)
         wait_twin(0, d1, LATE)
-        run(own_row, n0, pair_slot(0, d1), 1)
+        run(part(own_row, n0, pair_slot(0, d1), 1))
     pass_far(2)
+    for m in far_pairs:
+        wait_twin(*m, 0)
+    run(*[part(own_row, n0, pair_slot(*m), 1, 0, late) for m in far_pairs])
     pass_rest(1)
     pass_far(3)
-    for dl, d1 in far_pairs:
-        wait_twin(dl, d1, 0)
-        run(own_row, n0, pair_slot(dl, d1), 1, 0, late)
     pass_far(4)
-    for b in far_blocks:
-        run(b, 1, own_line, n1)
-    pass_rest(2)
-    for dl, d1 in far_pairs:
-        wait_twin(dl, d1, LATE)
-        for b in far_blocks:
-            run(b, 1, pair_slot(dl, d1), 1)
-        run(own_row, n0, pair_slot(dl, d1), 1, late)
-    pass_rest(3)
-    pass_rest(4)
-    for dh, d0 in rest_blocks:
-        wait_side(dh, d0, 0)
-        run(left_slot(dh, d0), 1, own_line, n1)
-        for m in far_pairs:
-            run(left_slot(dh, d0), 1, pair_slot(*m), 1)
-    for dl, d1 in rest_pairs:
-        wait_twin(dl, d1, 0)
-        wait_twin(dl, d1, LATE)
-        run(0, nleft, pair_slot(dl, d1), 1)
-
-    height = partial.shape[1]
-    lines = [
-        jnp.sum(sums_ref[slot, p], axis=0, keepdims=True) for slot in range(nleft) for p in range(npower)
-    ]
+    run(*[part(b, 1, own_line, n1) for b in far_blocks])
+    for m in far_pairs:
+        wait_twin(*m, LATE)
+    for m in rest_pairs:
+        wait_twin(*m, 0)
+    run(
+        *[part(b, 1, pair_slot(*m), 1) for b in far_blocks for m in far_pairs],
+        *[part(own_row, n0, pair_slot(*m), 1, late) for m in far_pairs],
+        *[part(own_row, n0, pair_slot(*m), 1, 0, late) for m in rest_pairs],
+        *[part(b, 1, pair_slot(*m), 1, 0, late) for b in far_blocks for m in rest_pairs],
+    )
+    for k in range(2, CHUNKS):
+        pass_rest(k)
+    for m in rest_blocks:
+        wait_side(*m, 0)
+    run(
+        *[part(left_slot(*b), 1, own_line, n1) for b in rest_blocks],
+        *[part(left_slot(*b), 1, pair_slot(*m), 1) for b in rest_blocks for m in far_pairs],
+        *[part(left_slot(*b), 1, pair_slot(*m), 1, 0, late) for b in rest_blocks for m in rest_pairs],
+    )
+    for m in rest_pairs:
+        wait_twin(*m, LATE)
+    for m in rest_pairs:
+        multiply(0, nleft, pair_slot(*m), 1, late)
+    for m in rest_pairs:
+        add(own_row, n0, pair_slot(*m), 1, late)
+    send_partials(early_blocks)
+    for m in rest_pairs:
+        for b in far_rows:
+            add(b, n0, pair_slot(*m), 1, late)
+
+    send_partials(late_blocks)
+    for group, sem in ((early_blocks, 1), (late_blocks, 2)):
+        if group:
+            count = (nleft - 1) * len(group)
+            remote(partial.at[pl.ds(0, count)], part_sem.at[0], part_sem.at[sem], dict(other=True)).wait_recv()
+    lines = []
+    for dh in range(nh):
+        for d0 in range(n0):
+            total = partial[index_of(0, 0, dh, d0)]
+            for a in range(nh):
+                for b in range(n0):
+                    if a or b:
+                        total = total + partial[index_of(a, b, (dh - a) % nh, (d0 - b) % n0)]
+            lines.append(total)
+    mine = lines[0]
+    height = degrees.shape[1]
     if height > nleft * npower:
         lines.append(jnp.zeros((height - nleft * npower, genes), jnp.float32))
-    partial[own_left] = jnp.concatenate(lines, axis=0)
-
-    mine_part = partial.at[own_left]
-    for dh in reversed(range(nh)):
-        for d0 in reversed(range(n0)):
-            if dh or d0:
-                remote(mine_part, part_sem.at[0], part_sem.at[1], dict(dh=dh, d0=d0)).start()
-    others = partial.at[pl.ds(0, nleft - 1)]
-    remote(others, part_sem.at[0], part_sem.at[1], dict(other=True)).wait_recv()
-    total = partial[0]
-    for slot in range(1, nleft):
-        total = total + partial[slot]
+    total = jnp.concatenate(lines, axis=0)
     own = own_pair * 2 + core
     degrees[own] = total
 
@@ -330,14 +371,14 @@
             for o in (True, False):
                 if dl or d1 or o:
                     remote(degrees.at[own], deg_sem.at[0], deg_sem.at[1], dict(dl=dl, d1=d1, other=o)).start()
-    mine = total[:npower]
-    for slot in range(1, nleft):
-        mine = jnp.where(own_left == slot, total[slot * npower:(slot + 1) * npower], mine)
     log_degree_ref[...] = jnp.log(mine) * LOG10E
 
-    for kind, a, b in flows:
-        remote(block, *sems(kind, a, b, 0), dict(other=True)).wait_send()
+    pair_flows = [flow for flow in flows if flow[0] in ("up", "twin")]
+    pairs_ref = right.reshape(2 * npair, genes, samples)
+    for group in ([flow for flow in flows if flow not in pair_flows], pair_flows):
+        remote(pairs_ref.at[pl.ds(0, len(group))], *sems(*group[0], 0), dict(other=True)).wait_send()
     remote(stats.at[pl.ds(0, len(flows))], *sems(*flows[0], STATS), dict(other=True)).wait_send()
+    others = partial.at[pl.ds(0, (nleft - 1) * nleft)]
     remote(others, part_sem.at[0], part_sem.at[1], dict(other=True)).wait_send()
     rest = degrees.at[pl.ds(0, 2 * npair - 1)]
     remote(rest, deg_sem.at[0], deg_sem.at[1], dict(other=True)).wait_recv()
@@ -382,16 +423,14 @@
     freq = freq / genes_all
     fit_ref[0:padded, :] = freq
     mean_log = jnp.log(totals[BINS] / genes_all) * LOG10E
-    inside = lane < BINS
-    xfit = jnp.log((lane.astype(jnp.float32) + 0.5) * peak / BINS) * LOG10E
+    logs = [math.log10(b + 0.5) for b in range(BINS)]
+    deviations = [value - sum(logs) / BINS for value in logs]
+    scale = sum(value * value for value in deviations)
+    xdev = jnp.zeros((padded, 128), jnp.float32)
+    for b in range(BINS):
+        xdev = jnp.where(lane == b, deviations[b] / scale, xdev)
     yfit = jnp.log(freq + 1.0 / genes_all) * LOG10E
-
-    def deviation(values):
-        mean = jnp.sum(jnp.where(inside, values, 0.0), axis=1, keepdims=True) / BINS
-        return jnp.where(inside, values - mean, 0.0)
-
-    xdev, ydev = deviation(xfit), deviation(yfit)
-    slope = jnp.sum(xdev * ydev, axis=1, keepdims=True) / jnp.sum(xdev * xdev, axis=1, keepdims=True)
+    slope = jnp.sum(xdev * yfit, axis=1, keepdims=True)
     on_line = jnp.logical_and(lane == line, line < npower)
     fit_ref[padded:padded + 1, :] = jnp.sum(jnp.where(on_line, slope, 0.0), axis=0, keepdims=True)
     fit_ref[padded + 1:padded + 2, :] = jnp.sum(jnp.where(on_line, mean_log, 0.0), axis=0, keepdims=True)
@@ -423,8 +462,8 @@
         log_degree, packed = pl.pallas_call(
             functools.partial(kernel, n0, n1, nh, nl, npower),
             out_shape=(
-                jax.ShapeDtypeStruct((npower, genes), f32),
-                jax.ShapeDtypeStruct((padded + 8, 128), f32),
+                pltpu.VMEM((npower, genes), f32),
+                pltpu.VMEM((padded + 8, 128), f32),
             ),
             in_specs=[hbm, hbm],
             out_specs=(vmem, vmem),
@@ -437,26 +476,21 @@
                 pltpu.VMEM((npair, 2 * genes, 128), f32),
                 pltpu.VMEM((nleft, npair, 2 * genes, genes), f32),
                 pltpu.VMEM((nleft, npower, 8, genes), f32),
-                pltpu.VMEM((nleft, height, genes), f32),
+                pltpu.VMEM((nleft * nleft, npower, genes), f32),
                 pltpu.VMEM((2 * npair, height, genes), f32),
                 dma((3,)),
-                dma((nh - 1,)),
-                dma((nh, n0 - 1)),
-                dma((nl - 1,)),
-                dma((nl, n1 - 1)),
-                dma((nl, n1)),
-                dma((1,)),
+                dma((3,)),
                 dma((nh - 1, CHUNKS)),
                 dma((nh, n0 - 1)),
                 dma((nl - 1, CHUNKS)),
                 dma((nl, n1 - 1, CHUNKS)),
                 dma((nl, n1, 2)),
                 dma((nleft + 2 * npair - 2,)),
-                dma((2,)),
+                dma((3,)),
                 dma((2,)),
             ],
             compiler_params=pltpu.CompilerParams(
-                collective_id=0, has_side_effects=True, vmem_limit_bytes=67043328
+                collective_id=0, has_side_effects=True, vmem_limit_bytes=67043328 - 128 * 1024
             ),
         )(powers, expression)
         log_degree, freq, slope, mean_log = pl.pallas_call(
@@ -469,6 +503,7 @@
             ),
             in_specs=[vmem, vmem],
             out_specs=(vmem,) * 4,
+            compiler_params=pltpu.CompilerParams(vmem_limit_bytes=1 << 20),
         )(log_degree, packed)
         return log_degree, freq, slope.reshape(npower), mean_log.reshape(npower)
 

time: 36.7 us -> 33.9 us (0.924)
  Pallas kernels: 35.8 us -> 33.1 us
    pallas_call x1, Pallas kernels: 34.5 us -> 32.5 us  [on_device(): pl.pallas_call(functools.partial(kernel, n0, n1, nh, nl, npower), out_sha...]
    pallas_call x1, Pallas kernels: 1.33 us -> 0.61 us  [on_device(): pl.pallas_call(functools.partial(unpack_kernel, npower), out_shape=(jax.S...]
where the time goes in v2:
time: 33.9 us; the launch traced here: 33.7 us
  Pallas kernels  33.1 us (98%)
  between operations  0.64 us (2%)
    pallas_call x1, Pallas kernels, on_device(): pl.pallas_call(functools.partial(kernel, n0, n1, nh, nl, npower), out_sha...  32.5 us

profile of v2, /device:TPU:0, one launch (start us, length us, event | category | flops | bytes accessed | tf_op | source)
XLA Modules:
  0.0 33.7 jit_solution(10334416127124334440)
XLA Ops:
  0.6 32.5 %shard_map.57 = (f32[10,128]{1,0:T(8,128)S(1)}, f32[24,128]{1,0:T(8,128)S(1)}) custom-call(s32[10]{0:T(128)} %powers_hbm.1, bf16[128,1024]{1,0:T(8,128)(2,1)} %expr_hbm.1), custom_call_target="tpu_custom_call" | custom-call | tf_op jit(solution)/shard_map/pallas_call | solution.py:462
  33.1 0.6 %shard_map.58 = (f32[10,128]{1,0:T(8,128)}, f32[10,10]{1,0:T(8,128)}, f32[1,10]{1,0:T(1,128)}, f32[1,10]{1,0:T(1,128)}) custom-call(f32[10,128]{1,0:T(8,128)S(1)} %get-tuple-element.10.log_degree_in, f32[24,128]{1,0:T(8,128)S(1)} %get-tuple-element.11.fit_in), custom_call_target="tpu_custom_call" | custom-call | tf_op jit(solution)/shard_map/pallas_call | solution.py:496

commit v3 on v2

--- a/solution.py
+++ b/solution.py
@@ -14,6 +14,7 @@
 LATE = 2
 STATS = CHUNKS
 STRIP = 32
+UNROLL = 2
 LOG2E = math.log2(math.e)
 LOG10E = math.log10(math.e)
 MESH = pl.DeviceIdType.MESH
@@ -63,15 +64,15 @@
         size = edges[k + 1] - edges[k]
         return right.at[slot, pl.ds(2 * edges[k] + side * size, size)]
 
+    for k in range(CHUNKS):
+        source = expr_hbm.at[pl.ds(edges[k], edges[k + 1] - edges[k])]
+        pltpu.make_async_copy(source, right_piece(own_pair, core, k), load_sem.at[0 if k == 0 else 1]).start()
     loads = [
-        pltpu.make_async_copy(expr_hbm, block, load_sem.at[0]),
-        pltpu.make_async_copy(powers_hbm, powers_ref, load_sem.at[1]),
+        pltpu.make_async_copy(expr_hbm, block, load_sem.at[2]),
+        pltpu.make_async_copy(powers_hbm, powers_ref, load_sem.at[3]),
     ]
     for load in loads:
         load.start()
-    for k in range(CHUNKS):
-        source = expr_hbm.at[pl.ds(edges[k], edges[k + 1] - edges[k])]
-        pltpu.make_async_copy(source, right_piece(own_pair, core, k), load_sem.at[2]).start()
 
     barrier = pltpu.get_barrier_semaphore()
     greeted = [dict(other=True)]
@@ -82,29 +83,16 @@
     for where in greeted:
         pl.semaphore_signal(barrier, inc=1, device_id=device(**where), device_id_type=MESH)
 
-    loads.append(pltpu.make_async_copy(expr_hbm, block, load_sem.at[2]))
-    for load in loads:
-        load.wait()
-
-    values = left[own_left].astype(jnp.float32)
-    mean = jnp.mean(values, axis=1, keepdims=True)
-    centred = values - mean
-    inv = lax.rsqrt(jnp.mean(centred * centred, axis=1, keepdims=True) + 1e-06)
-    own_stats = jnp.concatenate(
-        [jnp.broadcast_to(mean, (genes, 128)).T[0:1, :], jnp.broadcast_to(inv, (genes, 128)).T[0:1, :]], axis=0
-    )
-    stats[own_left] = own_stats
-    stats[nleft + own_pair * 2 + core] = own_stats
-    for slot in range(nleft):
-        for p in range(npower):
-            sums_ref[slot, p] = jnp.zeros((8, genes), jnp.float32)
-    exponents = [powers_ref[p].astype(jnp.float32) * LOG2E for p in range(npower)]
-
+    def load_wait(low, high, sem):
+        window = pl.ds(edges[low], edges[high] - edges[low])
+        pltpu.make_async_copy(expr_hbm.at[window], left.at[own_left, window], load_sem.at[sem]).wait()
+
+    load_wait(0, 1, 0)
     pl.semaphore_wait(barrier, len(greeted))
 
-    def remote(ref, send, recv, where):
+    def remote(ref, send, recv, where, src=None):
         return pltpu.make_async_remote_copy(
-            src_ref=ref, dst_ref=ref, send_sem=send, recv_sem=recv, device_id=device(**where), device_id_type=MESH
+            src_ref=ref if src is None else src, dst_ref=ref, send_sem=send, recv_sem=recv, device_id=device(**where), device_id_type=MESH
         )
 
     flows = [("far", dh, 0) for dh in range(1, nh)] + [("near", dl, 0) for dl in range(1, nl)]
@@ -136,7 +124,8 @@
             ref, where = right_piece(pair_slot(a, 0), core, k), dict(d1=b)
         else:
             ref, where = right_piece(pair_slot(a, b), core, k), dict(other=True)
-        remote(ref, *sems(kind, a, b, k), where).start()
+        own = right_piece(own_pair, core, k) if kind == "far" or (kind == "side" and a == 0) else None
+        remote(ref, *sems(kind, a, b, k), where, own).start()
 
     def wait(kind, a, b, k, ref):
         remote(ref, *sems(kind, a, b, k), dict(other=True)).wait_recv()
@@ -161,7 +150,7 @@
             ref = right.at[slot, pl.ds(0, edges[LATE]) if k < LATE else pl.ds(late, genes - edges[LATE])]
         wait("twin", dl, d1, k, ref)
 
-    for k in (STATS, *range(CHUNKS)):
+    def send_own(k):
         for first in (0, 1):
             @pl.when(core == first)
             def _():
@@ -174,6 +163,26 @@
         for d1 in range(1, n1):
             send("up", 0, d1, k)
         send("twin", 0, 0, k)
+
+    send_own(0)
+    load_wait(1, CHUNKS, 1)
+    for load in loads:
+        load.wait()
+    values = left[own_left].astype(jnp.float32)
+    mean = jnp.mean(values, axis=1, keepdims=True)
+    centred = values - mean
+    inv = lax.rsqrt(jnp.mean(centred * centred, axis=1, keepdims=True) + 1e-06)
+    own_stats = jnp.concatenate(
+        [jnp.broadcast_to(mean, (genes, 128)).T[0:1, :], jnp.broadcast_to(inv, (genes, 128)).T[0:1, :]], axis=0
+    )
+    stats[own_left] = own_stats
+    stats[nleft + own_pair * 2 + core] = own_stats
+    for k in (STATS, *range(1, CHUNKS)):
+        send_own(k)
+    for slot in range(nleft):
+        for p in range(npower):
+            sums_ref[slot, p] = jnp.zeros((8, genes), jnp.float32)
+    exponents = [powers_ref[p].astype(jnp.float32) * LOG2E for p in range(npower)]
 
     def multiply(ls, blocks, ps, pairs, lo=0, hi=2 * genes):
         size = hi - lo
@@ -202,9 +211,10 @@
         return ls, blocks, ps, pairs, lo, hi
 
     def run(*parts):
-        for each in parts:
-            multiply(*each)
-        for each in parts:
+        multiply(*parts[0])
+        for each, later in zip(parts, parts[1:] + (None,)):
+            if later is not None:
+                multiply(*later)
             add(*each)
 
     def add(ls, blocks, ps, pairs, lo=0, hi=2 * genes):
@@ -212,7 +222,11 @@
             accumulate(ls + lax.rem(u, blocks), ps + lax.div(u, blocks), lo, hi)
             return 0
 
-        lax.fori_loop(0, blocks * pairs, body, 0)
+        if blocks * pairs <= 4:
+            for u in range(blocks * pairs):
+                accumulate(ls + u % blocks, ps + u // blocks, lo, hi)
+        else:
+            lax.fori_loop(0, blocks * pairs, body, 0, unroll=UNROLL)
 
     def columns(dl, d1):
         slot = pair_slot(dl, d1)
@@ -245,15 +259,16 @@
             slot = left_slot(*m)
             rows = [jnp.sum(sums_ref[slot, p], axis=0, keepdims=True) for p in range(npower)]
             partial[index_of(0, 0, *m)] = jnp.concatenate(rows, axis=0)
+        first, count = index_of(0, 0, *group[0]), len(group)
         for a in reversed(range(nh)):
             for b in reversed(range(n0)):
-                for m in group:
-                    if a or b:
-                        pltpu.make_async_remote_copy(
-                            src_ref=partial.at[index_of(0, 0, *m)], dst_ref=partial.at[index_of(a, b, *m)],
-                            send_sem=part_sem.at[0], recv_sem=part_sem.at[1 if group is early_blocks else 2],
-                            device_id=device(dh=a, d0=b), device_id_type=MESH,
-                        ).start()
+                if a or b:
+                    pltpu.make_async_remote_copy(
+                        src_ref=partial.at[pl.ds(first, count)],
+                        dst_ref=partial.at[pl.ds(index_of(a, b, *group[0]), count)],
+                        send_sem=part_sem.at[0], recv_sem=part_sem.at[1 if group is early_blocks else 2],
+                        device_id=device(dh=a, d0=b), device_id_type=MESH,
+                    ).start()
 
     def pass_up(k):
         for d1 in range(1, n1):
@@ -280,39 +295,43 @@
     wait_twin(0, 0, 0)
     wait_twin(0, 0, LATE)
     columns(0, 0)
+    pass_up(0)
     pass_up(STATS)
-    pass_far(STATS)
-    pass_up(0)
     pass_up(1)
     pass_far(0)
-    pass_rest(STATS)
-    pass_up(2)
-    pass_up(3)
-    for dl in range(nl):
-        for d1 in range(n1):
-            if dl or d1:
-                wait_twin(dl, d1, STATS)
-                columns(dl, d1)
-    for dh in range(nh):
-        for d0 in range(1, n0):
-            wait_side(dh, d0, STATS)
-    pass_up(4)
+    pass_far(STATS)
+    for k in range(2, CHUNKS):
+        pass_up(k)
+    for d1 in range(1, n1):
+        wait_twin(0, d1, STATS)
+        columns(0, d1)
+    for d0 in range(1, n0):
+        wait_side(0, d0, STATS)
+        wait_side(0, d0, 0)
     pass_far(1)
-    for d0 in range(1, n0):
-        wait_side(0, d0, 0)
     run(part(own_row, n0, own_pair, 1))
-    pass_rest(0)
     for d1 in range(1, n1):
         wait_twin(0, d1, 0)
         wait_twin(0, d1, LATE)
         run(part(own_row, n0, pair_slot(0, d1), 1))
+    pass_rest(STATS)
+    pass_rest(0)
     pass_far(2)
     for m in far_pairs:
+        wait_twin(*m, STATS)
+        columns(*m)
         wait_twin(*m, 0)
     run(*[part(own_row, n0, pair_slot(*m), 1, 0, late) for m in far_pairs])
+    for m in rest_pairs:
+        wait_twin(*m, STATS)
+        columns(*m)
+    for dh in range(1, nh):
+        for d0 in range(1, n0):
+            wait_side(dh, d0, STATS)
     pass_rest(1)
     pass_far(3)
-    pass_far(4)
+    for k in range(4, CHUNKS):
+        pass_far(k)
     run(*[part(b, 1, own_line, n1) for b in far_blocks])
     for m in far_pairs:
         wait_twin(*m, LATE)
@@ -388,52 +407,47 @@
 
 def fit(genes_all, nleft, npower, degrees, fit_ref):
     blocks, height, genes = degrees.shape
-    padded = npower + 8 - npower % 8
-    spare = height - nleft * npower
+    padded = fit_ref.shape[0] - 8
 
     def fold(values, combine):
         total = values[:npower]
         for block in range(1, nleft):
             total = combine(total, values[block * npower:(block + 1) * npower])
-        return jnp.concatenate([total, jnp.ones((padded - npower, 1), jnp.float32)], axis=0)
-
-    best = lax.fori_loop(1, blocks, lambda index, best: jnp.maximum(best, degrees[index]), degrees[0])
-    peak = fold(jnp.max(best, axis=1, keepdims=True), jnp.maximum)
-    scales = [(BINS / peak)[:npower]] * nleft
-    if spare:
-        scales.append(jnp.ones((spare, 1), jnp.float32))
-    scale = jnp.broadcast_to(jnp.concatenate(scales, axis=0), (height, genes))
-
-    def weigh(index, carry):
-        carry = list(carry)
-        degree = degrees[index]
-        position = jnp.clip(degree * scale - 0.5, 0.0, BINS - 1.0)
-        for b in range(BINS):
-            carry[b] = carry[b] + jnp.maximum(0.0, 1.0 - jnp.abs(position - b))
-        carry[BINS] = carry[BINS] + degree
-        return tuple(carry)
-
-    totals = lax.fori_loop(0, blocks, weigh, tuple(jnp.zeros((height, genes), jnp.float32) for _ in range(BINS + 1)))
-    totals = [fold(jnp.sum(total, axis=1, keepdims=True), jnp.add) for total in totals]
-    lane = lax.broadcasted_iota(jnp.int32, (padded, 128), 1)
-    line = lax.broadcasted_iota(jnp.int32, (padded, 128), 0)
-    freq = jnp.zeros((padded, 128), jnp.float32)
-    for b in range(BINS):
-        freq = jnp.where(lane == b, totals[b], freq)
-    freq = freq / genes_all
-    fit_ref[0:padded, :] = freq
-    mean_log = jnp.log(totals[BINS] / genes_all) * LOG10E
+        return total
+
+    best = degrees[0]
+    for index in range(1, blocks):
+        best = jnp.maximum(best, degrees[index])
+    best = jnp.broadcast_to(jnp.max(best, axis=1, keepdims=True), (height, genes))
+    scales = [BINS / fold(best, jnp.maximum)] * nleft
+    if height > nleft * npower:
+        scales.append(jnp.ones((height - nleft * npower, genes), jnp.float32))
+    scale = jnp.concatenate(scales, axis=0)
+    positions = [jnp.clip(degrees[index] * scale - 0.5, 0.0, BINS - 1.0) for index in range(blocks)]
+    lane = lax.broadcasted_iota(jnp.int32, (height, 128), 1)
+    table = jnp.zeros((height, 128), jnp.float32)
+    for b in range(BINS + 1):
+        total = None
+        for index in range(blocks):
+            term = degrees[index] if b == BINS else jnp.maximum(0.0, 1.0 - jnp.abs(positions[index] - b))
+            total = term if total is None else total + term
+        table = jnp.where(lane == b, jnp.sum(total, axis=1, keepdims=True), table)
+    table = fold(table, jnp.add) / genes_all
+    fit_ref[0:npower, :] = table
+    lane = lax.broadcasted_iota(jnp.int32, (npower, 128), 1)
+    line = lax.broadcasted_iota(jnp.int32, (npower, 128), 0)
     logs = [math.log10(b + 0.5) for b in range(BINS)]
     deviations = [value - sum(logs) / BINS for value in logs]
-    scale = sum(value * value for value in deviations)
-    xdev = jnp.zeros((padded, 128), jnp.float32)
+    square = sum(value * value for value in deviations)
+    xdev = jnp.zeros((npower, 128), jnp.float32)
     for b in range(BINS):
-        xdev = jnp.where(lane == b, deviations[b] / scale, xdev)
-    yfit = jnp.log(freq + 1.0 / genes_all) * LOG10E
+        xdev = jnp.where(lane == b, deviations[b] / square, xdev)
+    yfit = jnp.log(jnp.where(lane < BINS, table + 1.0 / genes_all, 1.0)) * LOG10E
     slope = jnp.sum(xdev * yfit, axis=1, keepdims=True)
-    on_line = jnp.logical_and(lane == line, line < npower)
-    fit_ref[padded:padded + 1, :] = jnp.sum(jnp.where(on_line, slope, 0.0), axis=0, keepdims=True)
-    fit_ref[padded + 1:padded + 2, :] = jnp.sum(jnp.where(on_line, mean_log, 0.0), axis=0, keepdims=True)
+    total = jnp.sum(jnp.where(lane == BINS, table, 0.0), axis=1, keepdims=True)
+    mean_log = jnp.log(total) * LOG10E
+    fit_ref[padded:padded + 1, :] = jnp.sum(jnp.where(lane == line, slope, 0.0), axis=0, keepdims=True)
+    fit_ref[padded + 1:padded + 2, :] = jnp.sum(jnp.where(lane == line, mean_log, 0.0), axis=0, keepdims=True)
 
 
 def unpack_kernel(npower, log_degree_in, fit_in, log_degree_ref, freq_ref, slope_ref, mean_log_ref):
@@ -478,7 +492,7 @@
                 pltpu.VMEM((nleft, npower, 8, genes), f32),
                 pltpu.VMEM((nleft * nleft, npower, genes), f32),
                 pltpu.VMEM((2 * npair, height, genes), f32),
-                dma((3,)),
+                dma((4,)),
                 dma((3,)),
                 dma((nh - 1, CHUNKS)),
                 dma((nh, n0 - 1)),

time: 33.9 us -> 33.3 us (0.982)
  Pallas kernels: 33.1 us -> 32.6 us
    pallas_call x1, Pallas kernels: 32.5 us -> 31.9 us  [on_device(): pl.pallas_call(functools.partial(kernel, n0, n1, nh, nl, npower), out_sha...]
where the time goes in v3:
time: 33.3 us; the launch traced here: 33.2 us
  Pallas kernels  32.6 us (98%)
  between operations  0.64 us (2%)
    pallas_call x1, Pallas kernels, on_device(): pl.pallas_call(functools.partial(kernel, n0, n1, nh, nl, npower), out_sha...  31.9 us

profile of v3, /device:TPU:0, one launch (start us, length us, event | category | flops | bytes accessed | tf_op | source)
XLA Modules:
  0.0 33.2 jit_solution(15002050465296331983)
XLA Ops:
  0.6 31.9 %shard_map.57 = (f32[10,128]{1,0:T(8,128)S(1)}, f32[24,128]{1,0:T(8,128)S(1)}) custom-call(s32[10]{0:T(128)} %powers_hbm.1, bf16[128,1024]{1,0:T(8,128)(2,1)} %expr_hbm.1), custom_call_target="tpu_custom_call" | custom-call | tf_op jit(solution)/shard_map/pallas_call | solution.py:476
  32.6 0.6 %shard_map.58 = (f32[10,128]{1,0:T(8,128)}, f32[10,10]{1,0:T(8,128)}, f32[1,10]{1,0:T(1,128)}, f32[1,10]{1,0:T(1,128)}) custom-call(f32[10,128]{1,0:T(8,128)S(1)} %get-tuple-element.10.log_degree_in, f32[24,128]{1,0:T(8,128)S(1)} %get-tuple-element.11.fit_in), custom_call_target="tpu_custom_call" | custom-call | tf_op jit(solution)/shard_map/pallas_call | solution.py:510

commit v4 on v3

--- a/solution.py
+++ b/solution.py
@@ -27,7 +27,7 @@
 
 def kernel(
     n0, n1, nh, nl, npower, powers_hbm, expr_hbm, log_degree_ref, fit_ref,
-    powers_ref, left, right, stats, right_mean, right_inv, raw_ref, sums_ref, partial, degrees,
+    powers_ref, left, right, stats, right_mean, right_inv, raw_ref, sums_ref, partial, degrees, degrees_sent,
     load_sem, send_sem,
     far_recv, side_recv, near_recv, up_recv, twin_recv, stat_recv, part_sem, deg_sem,
 ):
@@ -251,24 +251,31 @@
     late_blocks = [(dh, d0) for dh in range(1, nh) for d0 in range(n0)]
     far_lines = [(cl + nl - dl) % nl * n1 for dl in range(1, nl)]
 
-    def index_of(a, b, dh, d0):
-        return (a * n0 + b) * nleft + dh * n0 + d0
+    def index_of(a, b, side, dh, d0):
+        return ((a * n0 + b) * 2 + side) * nleft + dh * n0 + d0
 
     def send_partials(group):
-        for m in group:
-            slot = left_slot(*m)
-            rows = [jnp.sum(sums_ref[slot, p], axis=0, keepdims=True) for p in range(npower)]
-            partial[index_of(0, 0, *m)] = jnp.concatenate(rows, axis=0)
-        first, count = index_of(0, 0, *group[0]), len(group)
-        for a in reversed(range(nh)):
-            for b in reversed(range(n0)):
-                if a or b:
-                    pltpu.make_async_remote_copy(
-                        src_ref=partial.at[pl.ds(first, count)],
-                        dst_ref=partial.at[pl.ds(index_of(a, b, *group[0]), count)],
-                        send_sem=part_sem.at[0], recv_sem=part_sem.at[1 if group is early_blocks else 2],
-                        device_id=device(dh=a, d0=b), device_id_type=MESH,
-                    ).start()
+        count = len(group)
+        blocks = [
+            jnp.concatenate([jnp.sum(sums_ref[left_slot(*m), p], axis=0, keepdims=True) for p in range(npower)], axis=0)
+            for m in group
+        ]
+        for side in (0, 1):
+            first = index_of(0, 0, side, *group[0])
+
+            @pl.when(core == side)
+            def _():
+                for i in range(count):
+                    partial[first + i] = blocks[i]
+                for a in reversed(range(nh)):
+                    for b in reversed(range(n0)):
+                        if a or b or side == 0:
+                            pltpu.make_async_remote_copy(
+                                src_ref=partial.at[pl.ds(first, count)],
+                                dst_ref=partial.at[pl.ds(index_of(a, b, side, *group[0]), count)],
+                                send_sem=part_sem.at[0], recv_sem=part_sem.at[1 if group is early_blocks else 2],
+                                device_id=device(dh=a, d0=b, other=side == 0), device_id_type=MESH,
+                            ).start()
 
     def pass_up(k):
         for d1 in range(1, n1):
@@ -364,45 +371,56 @@
             add(b, n0, pair_slot(*m), 1, late)
 
     send_partials(late_blocks)
-    for group, sem in ((early_blocks, 1), (late_blocks, 2)):
-        if group:
-            count = (nleft - 1) * len(group)
-            remote(partial.at[pl.ds(0, count)], part_sem.at[0], part_sem.at[sem], dict(other=True)).wait_recv()
-    lines = []
-    for dh in range(nh):
-        for d0 in range(n0):
-            total = partial[index_of(0, 0, dh, d0)]
-            for a in range(nh):
-                for b in range(n0):
-                    if a or b:
-                        total = total + partial[index_of(a, b, (dh - a) % nh, (d0 - b) % n0)]
-            lines.append(total)
-    mine = lines[0]
-    height = degrees.shape[1]
-    if height > nleft * npower:
-        lines.append(jnp.zeros((height - nleft * npower, genes), jnp.float32))
-    total = jnp.concatenate(lines, axis=0)
-    own = own_pair * 2 + core
-    degrees[own] = total
-
-    for dl in reversed(range(nl)):
-        for d1 in reversed(range(n1)):
-            for o in (True, False):
-                if dl or d1 or o:
-                    remote(degrees.at[own], deg_sem.at[0], deg_sem.at[1], dict(dl=dl, d1=d1, other=o)).start()
-    log_degree_ref[...] = jnp.log(mine) * LOG10E
+
+    @pl.when(core == 1)
+    def _():
+        for group, sem in ((early_blocks, 1), (late_blocks, 2)):
+            if group:
+                arrived = partial.at[pl.ds(0, (2 * nleft - 1) * len(group))]
+                remote(arrived, part_sem.at[0], part_sem.at[sem], dict(other=True)).wait_recv()
+        lines = []
+        for side in (0, 1):
+            for dh in range(nh):
+                for d0 in range(n0):
+                    total = None
+                    for a in range(nh):
+                        for b in range(n0):
+                            term = partial[index_of(a, b, side, (dh - a) % nh, (d0 - b) % n0)]
+                            total = term if total is None else total + term
+                    lines.append(total)
+        height = degrees.shape[1]
+        if height > 2 * nleft * npower:
+            lines.append(jnp.zeros((height - 2 * nleft * npower, genes), jnp.float32))
+        degrees[own_pair] = jnp.concatenate(lines, axis=0)
+        for dl in reversed(range(nl)):
+            for d1 in reversed(range(n1)):
+                for o in (True, False):
+                    if dl or d1 or o:
+                        where = dict(dl=dl, d1=d1, other=o)
+                        remote(degrees.at[own_pair], deg_sem.at[0], deg_sem.at[1], where).start()
 
     pair_flows = [flow for flow in flows if flow[0] in ("up", "twin")]
     pairs_ref = right.reshape(2 * npair, genes, samples)
     for group in ([flow for flow in flows if flow not in pair_flows], pair_flows):
         remote(pairs_ref.at[pl.ds(0, len(group))], *sems(*group[0], 0), dict(other=True)).wait_send()
     remote(stats.at[pl.ds(0, len(flows))], *sems(*flows[0], STATS), dict(other=True)).wait_send()
-    others = partial.at[pl.ds(0, (nleft - 1) * nleft)]
-    remote(others, part_sem.at[0], part_sem.at[1], dict(other=True)).wait_send()
-    rest = degrees.at[pl.ds(0, 2 * npair - 1)]
-    remote(rest, deg_sem.at[0], deg_sem.at[1], dict(other=True)).wait_recv()
-    fit(genes * nleft * npair * 2, nleft, npower, degrees, fit_ref)
-    remote(rest, deg_sem.at[0], deg_sem.at[1], dict(other=True)).wait_send()
+    for side in (0, 1):
+        @pl.when(core == side)
+        def _():
+            sent = partial.at[pl.ds(0, (nleft - side) * nleft)]
+            remote(sent, part_sem.at[0], part_sem.at[1], dict(other=True)).wait_send()
+            if npair > side:
+                arrived = degrees.at[pl.ds(0, npair - side)]
+                remote(arrived, deg_sem.at[0], deg_sem.at[1], dict(other=True)).wait_recv()
+
+    fit(genes * nleft * npair * 2, 2 * nleft, npower, degrees, fit_ref)
+    mine = degrees[own_pair, 0:npower]
+    mine = jnp.where(core == 1, degrees[own_pair, nleft * npower:(nleft + 1) * npower], mine)
+    log_degree_ref[...] = jnp.log(mine) * LOG10E
+
+    @pl.when(core == 1)
+    def _():
+        remote(degrees_sent.at[pl.ds(0, 2 * npair - 1)], deg_sem.at[0], deg_sem.at[1], dict(other=True)).wait_send()
 
 
 def fit(genes_all, nleft, npower, degrees, fit_ref):
@@ -467,7 +485,7 @@
         genes, samples = expression.shape
         npower = powers.shape[0]
         nleft, npair = nh * n0, nl * n1
-        height = -(-npower * nleft // 8) * 8
+        height = -(-2 * npower * nleft // 8) * 8
         vmem = pl.BlockSpec(memory_space=pltpu.VMEM)
         hbm = pl.BlockSpec(memory_space=pltpu.HBM)
         dma = pltpu.SemaphoreType.DMA
@@ -490,8 +508,9 @@
                 pltpu.VMEM((npair, 2 * genes, 128), f32),
                 pltpu.VMEM((nleft, npair, 2 * genes, genes), f32),
                 pltpu.VMEM((nleft, npower, 8, genes), f32),
-                pltpu.VMEM((nleft * nleft, npower, genes), f32),
-                pltpu.VMEM((2 * npair, height, genes), f32),
+                pltpu.VMEM((2 * nleft * nleft, npower, genes), f32),
+                pltpu.VMEM((npair, height, genes), f32),
+                pltpu.VMEM((2 * npair - 1, height, genes), f32),
                 dma((4,)),
                 dma((3,)),
                 dma((nh - 1, CHUNKS)),

time: 33.3 us -> 32.9 us (0.988)
  Pallas kernels: 32.6 us -> 32.1 us
    pallas_call x1, Pallas kernels: 31.9 us -> 31.5 us  [on_device(): pl.pallas_call(functools.partial(kernel, n0, n1, nh, nl, npower), out_sha...]
where the time goes in v4:
time: 32.9 us; the launch traced here: 32.8 us
  Pallas kernels  32.1 us (98%)
  between operations  0.64 us (2%)
    pallas_call x1, Pallas kernels, on_device(): pl.pallas_call(functools.partial(kernel, n0, n1, nh, nl, npower), out_sha...  31.5 us

profile of v4, /device:TPU:0, one launch (start us, length us, event | category | flops | bytes accessed | tf_op | source)
XLA Modules:
  0.0 32.8 jit_solution(651716379098858591)
XLA Ops:
  0.6 31.5 %shard_map.57 = (f32[10,128]{1,0:T(8,128)S(1)}, f32[24,128]{1,0:T(8,128)S(1)}) custom-call(s32[10]{0:T(128)} %powers_hbm.1, bf16[128,1024]{1,0:T(8,128)(2,1)} %expr_hbm.1), custom_call_target="tpu_custom_call" | custom-call | tf_op jit(solution)/shard_map/pallas_call | solution.py:494
  32.2 0.6 %shard_map.58 = (f32[10,128]{1,0:T(8,128)}, f32[10,10]{1,0:T(8,128)}, f32[1,10]{1,0:T(1,128)}, f32[1,10]{1,0:T(1,128)}) custom-call(f32[10,128]{1,0:T(8,128)S(1)} %get-tuple-element.10.log_degree_in, f32[24,128]{1,0:T(8,128)S(1)} %get-tuple-element.11.fit_in), custom_call_target="tpu_custom_call" | custom-call | tf_op jit(solution)/shard_map/pallas_call | solution.py:529

commit v5 on v4

--- a/solution.py
+++ b/solution.py
@@ -392,9 +392,9 @@
         if height > 2 * nleft * npower:
             lines.append(jnp.zeros((height - 2 * nleft * npower, genes), jnp.float32))
         degrees[own_pair] = jnp.concatenate(lines, axis=0)
-        for dl in reversed(range(nl)):
-            for d1 in reversed(range(n1)):
-                for o in (True, False):
+        for o in (True, False):
+            for dl in reversed(range(nl)):
+                for d1 in reversed(range(n1)):
                     if dl or d1 or o:
                         where = dict(dl=dl, d1=d1, other=o)
                         remote(degrees.at[own_pair], deg_sem.at[0], deg_sem.at[1], where).start()

time: 32.9 us -> 32.7 us (level)
    pallas_call x1, Pallas kernels: 31.5 us -> 31.2 us  [on_device(): pl.pallas_call(functools.partial(kernel, n0, n1, nh, nl, npower), out_sha...]
where the time goes in v5:
time: 32.7 us; the launch traced here: 32.5 us
  Pallas kernels  31.8 us (97%)
  between operations  0.64 us (2%)
    pallas_call x1, Pallas kernels, on_device(): pl.pallas_call(functools.partial(kernel, n0, n1, nh, nl, npower), out_sha...  31.2 us

profile of v5, /device:TPU:0, one launch (start us, length us, event | category | flops | bytes accessed | tf_op | source)
XLA Modules:
  0.0 32.5 jit_solution(14584548326333617839)
XLA Ops:
  0.6 31.2 %shard_map.57 = (f32[10,128]{1,0:T(8,128)S(1)}, f32[24,128]{1,0:T(8,128)S(1)}) custom-call(s32[10]{0:T(128)} %powers_hbm.1, bf16[128,1024]{1,0:T(8,128)(2,1)} %expr_hbm.1), custom_call_target="tpu_custom_call" | custom-call | tf_op jit(solution)/shard_map/pallas_call | solution.py:494
  31.8 0.6 %shard_map.58 = (f32[10,128]{1,0:T(8,128)}, f32[10,10]{1,0:T(8,128)}, f32[1,10]{1,0:T(1,128)}, f32[1,10]{1,0:T(1,128)}) custom-call(f32[10,128]{1,0:T(8,128)S(1)} %get-tuple-element.10.log_degree_in, f32[24,128]{1,0:T(8,128)S(1)} %get-tuple-element.11.fit_in), custom_call_target="tpu_custom_call" | custom-call | tf_op jit(solution)/shard_map/pallas_call | solution.py:529
